TPU v7x, 128 devices: a whole 4x4x4 slice. The times are simulated.
128 devices in a mesh: row: 4 (over x_hi, core), col: 32 (over y, z, x_lo).
Axes of the slice: x: 4 (x_hi: 2, x_lo: 2; x = x_hi * 2 + x_lo), y: 4, z: 4, core: 2. Of those that a mesh axis runs over, the one named last changes fastest.
Arguments:
- panel: bfloat16 [3072, 98304], P('row', 'col'), may hold values from -0.01953125 to 0.01953125
- surface: bfloat16 [98304, 1024], P('col'), may hold values from -6 to 6
- flexibility: float32 [4, 768, 768], P('row'), may hold values from -0.21875 to 0.21875
- owner_map: int32 [24], replicated, may hold values from 0 to 23, each once
- adjacency: int32 [4, 2], P('row'), may hold values from 0 to 3, as said below
- live_rows: int32 [24], replicated, may hold values from 1 to 128, 2304 in all
Outputs:
- response: float32 [1024, 98304], P('row', 'col')
Inputs may be any that keep to these rules, and one draw needn't show every extreme that they name: `adjacency`: each substructure lists 2 different neighbours, never itself. `owner_map`: every slot receives exactly one mortar block. `live_rows`: the live rows add up to 2304 and some block is full.
All inputs are finite; a program needn't handle non-finite values.
Results may differ from a plain program's by a relative error of at most 0.0029.
Values may be sent and summed in bfloat16 or wider, within the bound.
No kernel may reach another device: no remote copies, remote signals or barrier semaphores. Data moves between devices by JAX's collectives and lax.ppermute only.
A program may use at most 128 MiB of HBM per device.

v0:
```python
import math

import jax
import jax.numpy as jnp
from jax import lax
from jax.sharding import PartitionSpec as P

MBLK = 128
ITERS = 2


DAMPING = 0.6
COUPLING = 0.5


def cut_along(array, dim, devices):
    lengths = array.shape
    pieces = array.reshape(*lengths[:dim], devices, lengths[dim] // devices, *lengths[dim + 1 :])
    return jnp.moveaxis(pieces, dim, 0)


def sum_at_owner(array, axis, dim):
    devices = lax.axis_size(axis)
    pieces = lax.all_to_all(cut_along(array, dim, devices), axis, 0, 0, tiled=True)
    return jnp.sum(pieces, axis=0)


def laid_out(pieces, dim):
    pieces = jnp.moveaxis(pieces, 0, dim)
    lengths = pieces.shape
    return pieces.reshape(*lengths[:dim], lengths[dim] * lengths[dim + 1], *lengths[dim + 2 :])


def from_everyone(array, axis):
    devices = lax.axis_size(axis)
    return lax.all_to_all(
        jnp.broadcast_to(array[None], (devices, *array.shape)), axis, 0, 0, tiled=True
    )


def gather_directly(array, axis, dim):
    return laid_out(from_everyone(array, axis), dim)


def live_pattern(live_rows):
    offsets = jnp.arange(MBLK, dtype=jnp.int32)
    return (offsets[None, :] < live_rows[:, None]).astype(jnp.float32)


def body(panel, surface, flexibility, owner_map, adjacency, live_rows):
    order_rows, column_count = panel.shape
    row_total = lax.axis_size("row")
    col_total = lax.axis_size("col")
    own_row = lax.axis_index("row")
    load_total = surface.shape[1]
    load_share = load_total // col_total
    block_count = order_rows // MBLK
    traction = sum_at_owner(
        lax.dot_general(
            surface, panel, (((0,), (1,)), ((), ())), preferred_element_type=jnp.float32
        ),
        "col",
        0,
    )
    pattern = live_pattern(live_rows)
    own_pattern = lax.dynamic_slice_in_dim(pattern, own_row * block_count, block_count, 0)
    blocks = traction.reshape(load_share, block_count, MBLK) * own_pattern[None]
    every_block = gather_directly(blocks, "row", 1)
    block_total = owner_map.shape[0]
    inverse = (
        jnp.zeros((block_total,), jnp.int32)
        .at[owner_map]
        .set(jnp.arange(block_total, dtype=jnp.int32))
    )
    own_sources = lax.dynamic_slice_in_dim(inverse, own_row * block_count, block_count, 0)
    load_blocks = jnp.take(every_block, own_sources, axis=1).reshape(load_share, order_rows)
    hits = adjacency[0][:, None] == jnp.arange(row_total, dtype=jnp.int32)[None, :]
    neighbour_weights = jnp.sum(hits.astype(jnp.float32), axis=0)
    flex_local = flexibility[0]
    traces = jnp.zeros_like(load_blocks)
    for sweep_index in range(ITERS):
        coupled = load_blocks
        if sweep_index > 0:
            neighbours = gather_directly(traces[None], "row", 0)
            coupled = load_blocks + COUPLING * jnp.einsum(
                "n,nlo->lo", neighbour_weights, neighbours, precision=lax.Precision.HIGHEST
            )
        applied = lax.dot_general(
            coupled,
            flex_local,
            (((1,), (1,)), ((), ())),
            precision=lax.Precision.HIGHEST,
            preferred_element_type=jnp.float32,
        )
        traces = (1.0 - DAMPING) * traces + DAMPING * applied
    rounded = traces.astype(jnp.bfloat16).reshape(load_share, block_count, MBLK)
    every_trace = lax.all_gather(rounded, "row", axis=1, tiled=True)
    own_slots = lax.dynamic_slice_in_dim(owner_map, own_row * block_count, block_count, 0)
    updated = (
        jnp.take(every_trace, own_slots, axis=1) * own_pattern[None].astype(jnp.bfloat16)
    ).reshape(load_share, order_rows)
    all_loads = gather_directly(updated, "col", 0)
    gain_factor = math.sqrt(column_count * col_total / (order_rows * row_total))
    return lax.psum_scatter(
        gain_factor * jnp.dot(all_loads, panel, preferred_element_type=jnp.float32),
        "row",
        scatter_dimension=0,
        tiled=True,
    )


def solution(mesh):
    in_specs = (P("row", "col"), P("col", None), P("row", None, None), P(), P("row", None), P())
    out_specs = P("row", "col")
    return jax.shard_map(body, mesh=mesh, in_specs=in_specs, out_specs=out_specs, check_vma=False)
```

profile of v0, /device:TPU:1, one launch (start us, length us, event | category | flops | bytes accessed | tf_op | source)
XLA Modules:
  0.0 264.3 jit_solution(17379969602738920480)
XLA Ops:
  6.5 0.0 copy-start
  6.5 9.9 %fusion.36 = f32[1024,768]{1,0:T(8,128)} fusion(bf16[3072,1024]{1,0:T(8,128)(2,1)} %param.7, bf16[768,3072]{1,0:T(8,128)(2,1)} %param.6), kind=kOutput, calls=%fused_computation.50 | convolution fusion | flops 4831838208 | bytes 14155776 | tf_op jit(solution)/shard_map/dot_general | solution.py:59
  16.4 10.1 %all-to-all-start = ((f32[32,32,768]{2,1,0:T(8,128)}), f32[32,32,768]{2,1,0:T(8,128)}, u32[]{:S(2)}, u32[]{:S(2)}) async-start(f32[32,32,768]{2,1,0:T(8,128)} %bitcast.78), calls=%async_computation | async-start | bytes 6291456 | tf_op jit(solution)/shard_map/all_to_all | solution.py:24
  26.5 0.0 copy-done.2
  26.5 0.1 dynamic-slice
  26.6 0.6 scatter_custom_fusion
  27.3 0.1 compare_and_fusion
  27.4 0.1 fusion.30
  27.5 0.1 convert_bitcast_fusion
  27.5 46.6 %all-to-all-done = f32[32,32,768]{2,1,0:T(8,128)} async-done(((f32[32,32,768]{2,1,0:T(8,128)}), f32[32,32,768]{2,1,0:T(8,128)}, u32[]{:S(2)}, u32[]{:S(2)}) %all-to-all-start) | async-done | bytes 3145760 | tf_op jit(solution)/shard_map/all_to_all | solution.py:24
  74.1 2.1 reduce_sum.18
  76.3 0.8 broadcast_in_dim.65
  77.0 5.9 %all-to-all-start.1 = ((f32[4,32,6,128]{3,1,2,0:T(8,128)}), f32[4,32,6,128]{3,1,2,0:T(8,128)S(1)}, u32[]{:S(2)}, u32[]{:S(2)}) async-start(f32[4,32,6,128]{3,1,2,0:T(8,128)} %broadcast_in_dim.65), calls=%async_computation.1 | async-start | bytes 786432 | tf_op jit(solution)/shard_map/all_to_all | solution.py:36
  82.9 0.1 compare_and_fusion.1
  83.0 0.1 broadcast_bitcast_fusion
  83.1 7.8 %all-to-all-done.1 = f32[4,32,6,128]{3,1,2,0:T(8,128)S(1)} async-done(((f32[4,32,6,128]{3,1,2,0:T(8,128)}), f32[4,32,6,128]{3,1,2,0:T(8,128)S(1)}, u32[]{:S(2)}, u32[]{:S(2)}) %all-to-all-start.1) | async-done | bytes 393248 | tf_op jit(solution)/shard_map/all_to_all | solution.py:36
  90.9 0.6 gather_fusion
  91.4 0.0 copy-done
  91.4 2.3 broadcast_multiply_fusion.1
  93.7 0.8 broadcast_in_dim.72
  94.5 4.4 %all-to-all-start.2 = ((f32[4,1,32,768]{3,2,1,0:T(8,128)}), f32[4,1,32,768]{3,2,1,0:T(8,128)S(1)}, u32[]{:S(2)}, u32[]{:S(2)}) async-start(f32[4,1,32,768]{3,2,1,0:T(8,128)} %broadcast_in_dim.72), calls=%async_computation.2 | async-start | bytes 786432 | tf_op jit(solution)/shard_map/all_to_all | solution.py:36
  98.9 0.1 broadcast_bitcast_fusion.1
  99.0 7.9 %all-to-all-done.2 = f32[4,1,32,768]{3,2,1,0:T(8,128)S(1)} async-done(((f32[4,1,32,768]{3,2,1,0:T(8,128)}), f32[4,1,32,768]{3,2,1,0:T(8,128)S(1)}, u32[]{:S(2)}, u32[]{:S(2)}) %all-to-all-start.2) | async-done | bytes 393248 | tf_op jit(solution)/shard_map/all_to_all | solution.py:36
  106.8 1.0 fusion.16
  107.8 2.2 fusion.13
  110.0 7.9 %all_gather.3 = bf16[32,24,128]{2,0,1:T(8,128)(2,1)S(1)} all-gather(bf16[32,6,128]{2,0,1:T(8,128)(2,1)S(1)} %bitcast.82), channel_id=1, replica_groups=mesh['row'=4,'col'=32] {'row'}, dimensions={1}, use_global_device_ids=true | all-gather | bytes 245760 | tf_op jit(solution)/shard_map/all_gather | solution.py:97
  118.0 0.6 gather_fusion.1
  118.5 0.2 broadcast_in_dim.75
  118.7 26.5 %all_to_all.20 = bf16[32,32,768]{2,1,0:T(8,128)(2,1)S(1)} all-to-all(bf16[32,32,768]{2,1,0:T(8,128)(2,1)S(1)} %broadcast_in_dim.75), channel_id=1, replica_groups=mesh['row'=4,'col'=32] {'col'}, dimensions={0} | all-to-all | bytes 3145728 | tf_op jit(solution)/shard_map/all_to_all | solution.py:36
  145.2 10.3 %convolution_multiply_fusion = f32[1024,3072]{1,0:T(8,128)} fusion(bf16[1024,768]{1,0:T(8,128)(2,1)S(1)} %bitcast.79, bf16[768,3072]{1,0:T(8,128)(2,1)} %param.6), kind=kOutput, calls=%fused_computation.3 | convolution fusion | flops 4834983936 | bytes 18874368 | tf_op jit(solution)/shard_map/dot_general | solution.py:105
  155.5 0.0 reduce-scatter.2.cloned.1.call-update
  155.5 101.9 %reduce-scatter.2.cloned.1.call-done = f32[256,3072]{1,0:T(8,128)} async-done(((f32[1024,3072]{1,0:T(8,128)}), f32[256,3072]{1,0:T(8,128)}) %reduce-scatter.2.cloned.1.call-update) | async-done | bytes 3145744 | tf_op jit(solution)/shard_map/reduce_scatter | solution.py:104
  (15 shorter events, 0.1 us)
Async XLA Ops:
  6.5 84.9 %copy-start = (f32[1,768,768]{2,1,0:T(8,128)S(1)}, f32[1,768,768]{2,1,0:T(8,128)}, u32[]{:S(2)}) copy-start(f32[1,768,768]{2,1,0:T(8,128)} %param.8) | copy-start | bytes 7077892
  16.4 10.1 %copy-start.2 = (s32[24]{0:T(128)S(1)}, s32[24]{0:T(128)}, u32[]{:S(2)}) copy-start(s32[24]{0:T(128)} %param.11) | copy-start | bytes 292
  16.4 10.2 %copy-start.1 = (s32[24]{0:T(128)S(1)}, s32[24]{0:T(128)}, u32[]{:S(2)}) copy-start(s32[24]{0:T(128)} %param.9) | copy-start | bytes 292
  16.4 10.9 %copy-start.3 = (s32[1,2]{1,0:T(1,128)S(1)}, s32[1,2]{1,0:T(1,128)}, u32[]{:S(2)}) copy-start(s32[1,2]{1,0:T(1,128)} %param.10) | copy-start | bytes 28
  16.4 57.7 %all-to-all-start = ((f32[32,32,768]{2,1,0:T(8,128)}), f32[32,32,768]{2,1,0:T(8,128)}, u32[]{:S(2)}, u32[]{:S(2)}) async-start(f32[32,32,768]{2,1,0:T(8,128)} %bitcast.78), calls=%async_computation | async-start | bytes 6291456 | tf_op jit(solution)/shard_map/all_to_all | solution.py:24
  77.0 13.8 %all-to-all-start.1 = ((f32[4,32,6,128]{3,1,2,0:T(8,128)}), f32[4,32,6,128]{3,1,2,0:T(8,128)S(1)}, u32[]{:S(2)}, u32[]{:S(2)}) async-start(f32[4,32,6,128]{3,1,2,0:T(8,128)} %broadcast_in_dim.65), calls=%async_computation.1 | async-start | bytes 786432 | tf_op jit(solution)/shard_map/all_to_all | solution.py:36
  94.5 12.4 %all-to-all-start.2 = ((f32[4,1,32,768]{3,2,1,0:T(8,128)}), f32[4,1,32,768]{3,2,1,0:T(8,128)S(1)}, u32[]{:S(2)}, u32[]{:S(2)}) async-start(f32[4,1,32,768]{3,2,1,0:T(8,128)} %broadcast_in_dim.72), calls=%async_computation.2 | async-start | bytes 786432 | tf_op jit(solution)/shard_map/all_to_all | solution.py:36
  98.9 158.6 %reduce-scatter.2.cloned.1.call-start = ((), (), s32[]{:S(2)}) async-start(), calls=%async_computation.5 | async-start | bytes 15728640 | tf_op jit(solution)/shard_map/reduce_scatter | solution.py:104
Sparse Core Ops, SparseCore 0:
  155.6 101.7 reduce-scatter.1
where the time goes:
time: 265 us; the launch traced here: 264 us
  waiting for transfers between devices  164 us (62%)
  blocking collectives  34.4 us (13%)
  matrix products  25.7 us (10%)
  starting transfers between devices  20.3 us (8%)
  between operations  13.5 us (5%)
  local copies, waits for them, and re-layouts  3.78 us (1%)
    reduce_scatter x1, waiting for transfers between devices, body(): lax.psum_scatter(gain_factor * jnp.dot(all_loads, panel, preferred_elemen...  102 us
    all_to_all x1, waiting for transfers between devices, sum_at_owner(): lax.all_to_all(cut_along(array, dim, devices), axis, 0, 0, tiled=True)  46.6 us
    all_to_all x1, blocking collectives, from_everyone(): lax.all_to_all(jnp.broadcast_to(array[None], (devices, *array.shape)), ax...  26.5 us
    all_to_all x2, waiting for transfers between devices, from_everyone(): lax.all_to_all(jnp.broadcast_to(array[None], (devices, *array.shape)), ax...  15.7 us
    dot_general x1, matrix products, body(): jnp.dot(all_loads, panel, preferred_element_type=jnp.float32)  10.3 us
    all_to_all x2, starting transfers between devices, from_everyone(): lax.all_to_all(jnp.broadcast_to(array[None], (devices, *array.shape)), ax...  10.3 us
    all_to_all x1, starting transfers between devices, sum_at_owner(): lax.all_to_all(cut_along(array, dim, devices), axis, 0, 0, tiled=True)  10.1 us
    dot_general x1, matrix products, body(): lax.dot_general(surface, panel, (((0,), (1,)), ((), ())), preferred_eleme...  9.9 us
  transfers between devices with their start and end apart: 4, of which 4 were waited for; matrix products, arithmetic and copies ran while one was open for 0% of the time, Pallas kernels for 0%

commit v1 on v0

v1 whole, which is shorter than its diff:
```python
import math

import jax
import jax.numpy as jnp
from jax import lax
from jax.experimental import pallas as pl
from jax.experimental.pallas import tpu as pltpu
from jax.sharding import PartitionSpec as P


MBLK = 128
ITERS = 2
DAMPING = 0.6
COUPLING = 0.5
PAD = 8
CHUNKS = 2
LISTED = 16.0
MIB = 1 << 20
PART_SCALE = 2048.0
FLEX_SCALE = 131072.0


def swap(array, flip):
    rows = lax.axis_size("row")
    return lax.ppermute(array, "row", [(i, i ^ flip) for i in range(rows)])


def far_swap(array, flip_row, flip_col):
    rows, cols = lax.axis_size("row"), lax.axis_size("col")
    pairs = [
        (r * cols + c, (r ^ flip_row) * cols + (c ^ flip_col)) for r in range(rows) for c in range(cols)
    ]
    return lax.ppermute(array, ("row", "col"), pairs)


def to_root(values, scale):
    return (scale * jnp.sign(values) * jnp.sqrt(jnp.abs(values))).astype(jnp.float16)


def from_root(roots, scale):
    roots = roots.astype(jnp.float32)
    return scale**-2 * (roots * jnp.abs(roots))


def split_in_two(values):
    high = lax.reduce_precision(values, 8, 7)
    return high.astype(jnp.bfloat16), (values - high).astype(jnp.bfloat16)


def planes():
    cols = lax.axis_size("col")
    return [list(range(low, cols, 2)) for low in range(2)]


def from_everyone(array, groups=None):
    devices = lax.axis_size("col") if groups is None else len(groups[0])
    return lax.all_to_all(
        jnp.broadcast_to(array[None], (devices, *array.shape)),
        "col",
        0,
        0,
        axis_index_groups=groups,
        tiled=True,
    )


def iterate(owner_ref, live_ref, me_ref, kept_ref, next_ref, far_ref, both_ref, *refs):
    stored = refs[0:8]
    here_ref, there_ref = refs[8:10]
    blocks_ref, loads_ref, slots_ref, inverse_ref, high_ref, low_ref, sems = refs[10:17]
    order = high_ref.shape[2]
    highs = [pltpu.make_async_copy(stored[i], high_ref.at[i], sems.at[i]) for i in range(4)]
    lows = [pltpu.make_async_copy(stored[4 + i], low_ref.at[i], sems.at[4 + i]) for i in range(4)]
    for s in range(4):
        highs[s].start()
        lows[s].start()
    half = kept_ref.shape[0]
    blocks_ref[:half] = kept_ref[...] + next_ref[...]
    blocks_ref[half:] = far_ref[...] + both_ref[...]
    me = me_ref[0]
    total = blocks_ref.shape[0]
    count = total // 4
    group = blocks_ref.shape[1]
    places = [me ^ flip for flip in range(4)]

    def place_of(block):
        return ((block // count) ^ me) * count + lax.rem(block, count)

    for b in range(total):
        inverse_ref[owner_ref[b]] = b
    lane = lax.broadcasted_iota(jnp.int32, (group, MBLK), 1)
    for s in range(4):
        for j in range(count):
            block = inverse_ref[places[s] * count + j]
            values = blocks_ref[place_of(block)]
            loads_ref[s, :, j * MBLK : (j + 1) * MBLK] = jnp.where(
                lane < live_ref[block], values, 0.0
            )

    def apply(values, s):
        high = values.astype(jnp.bfloat16)
        low = (values - high.astype(jnp.float32)).astype(jnp.bfloat16)
        dims = (((1,), (1,)), ((), ()))
        both = lax.dot_general(
            jnp.concatenate([high, low], axis=0),
            high_ref[s, :order],
            dims,
            preferred_element_type=jnp.float32,
        )
        rest = lax.dot_general(high, low_ref[s, :order], dims, preferred_element_type=jnp.float32)
        return both[:group] + both[group:] + rest

    traces = []
    for s in range(4):
        highs[s].wait()
        lows[s].wait()
        traces.append(DAMPING * apply(loads_ref[s], s))
    for _ in range(ITERS - 1):
        coupled = []
        for s in range(4):
            around = jnp.zeros_like(traces[0])
            for n in range(4):
                place = places[n].astype(jnp.float32)
                for k in range(2):
                    listed = high_ref[s, order + k * PAD : order + (k + 1) * PAD].astype(jnp.float32)
                    around = around + jnp.where(LISTED * listed == place, traces[n], 0.0)
            coupled.append(loads_ref[s] + COUPLING * around)
        traces = [
            (1.0 - DAMPING) * traces[s] + DAMPING * apply(coupled[s], s) for s in range(4)
        ]
    for s in range(4):
        for j in range(count):
            slots_ref[s * count + j] = traces[s][:, j * MBLK : (j + 1) * MBLK]
    for out_ref, pair in ((here_ref, (0, 1)), (there_ref, (2, 3))):
        for i, flip in enumerate(pair):
            for j in range(count):
                block = (me ^ flip) * count + j
                values = slots_ref[place_of(owner_ref[block])]
                values = jnp.where(lane < live_ref[block], values, 0.0).astype(jnp.bfloat16)
                if out_ref is there_ref:
                    out_ref[i * count + j] = values
                else:
                    for copy in range(out_ref.shape[0]):
                        out_ref[copy, i * count + j] = values


def body(panel, surface, flexibility, owner_map, adjacency, live_rows):
    order_rows, column_count = panel.shape
    row_total = lax.axis_size("row")
    col_total = lax.axis_size("col")
    own_row = lax.axis_index("row")
    load_total = surface.shape[1]
    block_count = order_rows // MBLK
    block_total = owner_map.shape[0]
    group = load_total // (row_total * col_total)

    flex_own = flexibility[0]
    lists = jnp.repeat(adjacency[0].astype(jnp.float32) / LISTED, PAD)
    flex_own = jnp.concatenate(
        [flex_own, jnp.broadcast_to(lists[:, None], (2 * PAD, order_rows))], axis=0
    )
    flex_packed = to_root(flex_own, FLEX_SCALE)
    flex_far = swap(flex_packed, 2)
    panel_beside = swap(panel, 1)
    surface, flex_packed, flex_own = lax.optimization_barrier((surface, flex_packed, flex_own))

    partial = lax.dot_general(
        surface, panel, (((0,), (1,)), ((), ())), preferred_element_type=jnp.float32
    )
    pieces = to_root(partial, PART_SCALE)
    pieces = pieces.reshape(row_total, col_total // 2, 2, group, block_count, MBLK)
    pieces = pieces.transpose(1, 2, 0, 4, 3, 5)
    pieces = pieces.reshape(col_total // 2, 2 * row_total * block_count * group, MBLK)
    received = lax.all_to_all(pieces, "col", 0, 0, axis_index_groups=planes(), tiled=True)
    received, panel_beside = lax.optimization_barrier((received, panel_beside))

    high, low = split_in_two(flex_own)
    far_high, far_low = split_in_two(from_root(flex_far, FLEX_SCALE))
    highs = [high, swap(high, 1), far_high, swap(far_high, 1)]
    lows = [low, swap(low, 1), far_low, swap(far_low, 1)]
    traction = jnp.sum(from_root(received, PART_SCALE), axis=0)

    own_far = own_row // 2
    own_core = own_row % 2
    own_low = lax.axis_index("col") % 2
    traction = traction.reshape(4, 2, block_count, group, MBLK)
    kept = lax.dynamic_index_in_dim(traction, own_core, 1, keepdims=False)
    sent = lax.dynamic_index_in_dim(traction, 1 - own_core, 1, keepdims=False)
    chip_rows = jnp.concatenate([kept, swap(sent, 1)], axis=1)

    def chip_part(low, far):
        return lax.dynamic_index_in_dim(chip_rows, low * 2 + far, 0, keepdims=False)

    from_far = far_swap(chip_part(own_low, own_far), 2, 0)
    from_next = far_swap(chip_part(1 - own_low, 1 - own_far), 0, 1)
    from_both = far_swap(chip_part(1 - own_low, own_far), 2, 1)

    smem = pl.BlockSpec(memory_space=pltpu.SMEM)
    vmem = pl.BlockSpec(memory_space=pltpu.VMEM)
    hbm = pl.BlockSpec(memory_space=pl.ANY)
    shape = (2 * block_count, group, MBLK)
    here, there = pl.pallas_call(
        iterate,
        out_shape=(
            jax.ShapeDtypeStruct((col_total, *shape), jnp.bfloat16),
            jax.ShapeDtypeStruct(shape, jnp.bfloat16),
        ),
        in_specs=[smem] * 3 + [vmem] * 4 + [hbm] * 8,
        out_specs=(vmem, vmem),
        scratch_shapes=[
            pltpu.VMEM((block_total, group, MBLK), jnp.float32),
            pltpu.VMEM((row_total, group, order_rows), jnp.float32),
            pltpu.VMEM((block_total, group, MBLK), jnp.float32),
            pltpu.SMEM((block_total,), jnp.int32),
            pltpu.VMEM((row_total, order_rows + 2 * PAD, order_rows), jnp.bfloat16),
            pltpu.VMEM((row_total, order_rows + 2 * PAD, order_rows), jnp.bfloat16),
            pltpu.SemaphoreType.DMA((8,)),
        ],
        cost_estimate=pl.CostEstimate(
            flops=2 * ITERS * row_total * group * order_rows**2 * 24,
            bytes_accessed=4 * row_total * order_rows**2,
            transcendentals=0,
        ),
        compiler_params=pltpu.CompilerParams(vmem_limit_bytes=20 * MIB),
        name="iterate",
    )(
        owner_map,
        live_rows,
        jnp.full((1,), own_row, jnp.int32),
        chip_part(own_low, 1 - own_far),
        from_next,
        from_far,
        from_both,
        *highs,
        *lows,
    )

    gain_factor = math.sqrt(column_count * col_total / (order_rows * row_total))

    def as_rows(everyones):
        values = everyones.reshape(col_total, 2 * block_count, group, MBLK).transpose(0, 2, 1, 3)
        return values.reshape(col_total * group, 2 * order_rows)

    width = column_count // CHUNKS
    cuts = [slice(i * width, (i + 1) * width) for i in range(CHUNKS)]

    def times_panel(values, cut):
        return gain_factor * (
            jnp.dot(values[:, :order_rows], panel[:, cut], preferred_element_type=jnp.float32)
            + jnp.dot(
                values[:, order_rows:], panel_beside[:, cut], preferred_element_type=jnp.float32
            )
        )

    lent_rows = as_rows(lax.all_to_all(here, "col", 0, 0, tiled=True))
    home, beyond = far_swap(there, 2, 0), far_swap(there, 2, 1)
    home = jnp.where(own_low == 0, jnp.stack([home, beyond]), jnp.stack([beyond, home]))
    away = []
    for cut in cuts:
        lent = times_panel(lent_rows, cut).astype(jnp.bfloat16)
        lent, lent_rows = lax.optimization_barrier((lent, lent_rows))
        away.append(swap(lent, 2))
    home_rows = as_rows(from_everyone(home, planes()))
    own = lax.optimization_barrier([times_panel(home_rows, cut) for cut in cuts])
    return jnp.concatenate([o + a.astype(jnp.float32) for o, a in zip(own, away)], axis=1)


def solution(mesh):
    in_specs = (P("row", "col"), P("col", None), P("row", None, None), P(), P("row", None), P())
    out_specs = P("row", "col")
    return jax.shard_map(body, mesh=mesh, in_specs=in_specs, out_specs=out_specs, check_vma=False)
```

time: 265 us -> 140 us (0.53)
  the two profiles are of different devices: /device:TPU:1 before, /device:TPU:0 now
where the time goes in v1:
time: 140 us; the launch traced here: 139 us
  waiting for transfers between devices  52.7 us (38%)
  starting transfers between devices  33 us (24%)
  matrix products  27.8 us (20%)
  other arithmetic  14.1 us (10%)
  Pallas kernels  8.62 us (6%)
  local copies, waits for them, and re-layouts  2.84 us (2%)
    ppermute x9, waiting for transfers between devices, swap(): return lax.ppermute(array, 'row', [(i, i ^ flip) for i in range(rows)])  26.8 us
    all_to_all x1, waiting for transfers between devices, body(): lax.all_to_all(pieces, 'col', 0, 0, axis_index_groups=planes(), tiled=True)  13 us
    dot_general x4, matrix products, times_panel(): jnp.dot(values[:, order_rows:], panel_beside[:, cut], preferred_element_t...  10.8 us
    ppermute x5, waiting for transfers between devices, far_swap(): return lax.ppermute(array, ('row', 'col'), pairs)  9.58 us
    ppermute x5, starting transfers between devices, far_swap(): return lax.ppermute(array, ('row', 'col'), pairs)  9.32 us
    dot_general x1, matrix products, body(): lax.dot_general(surface, panel, (((0,), (1,)), ((), ())), preferred_eleme...  8.74 us
    pallas_call x1, Pallas kernels, body(): pl.pallas_call(iterate, out_shape=(jax.ShapeDtypeStruct((col_total, *shap...  8.62 us
    dot_general x4, matrix products, times_panel(): jnp.dot(values[:, :order_rows], panel[:, cut], preferred_element_type=jnp...  8.22 us
  transfers between devices with their start and end apart: 17, of which 9 were waited for; matrix products, arithmetic and copies ran while one was open for 29% of the time, Pallas kernels for 0%

profile of v1, /device:TPU:0, one launch (start us, length us, event | category | flops | bytes accessed | tf_op | source)
XLA Modules:
  0.0 139.3 jit_solution(8988945438959625415)
XLA Ops:
  0.8 4.4 %pad_maximum_fusion.1 = (f32[784,768]{1,0:T(8,128)S(1)}, f16[784,768]{1,0:T(8,128)(2,1)}) fusion(f32[768,768]{1,0:T(8,128)} %bitcast.38, f32[784]{0:T(1024)S(1)} %pad.9.clone), kind=kLoop, calls=%fused_computation.23 | loop fusion | flops 3612672 | bytes 5975104 | tf_op jit(solution)/shard_map/concatenate | solution.py:159
  5.3 3.1 %collective-permute-start.6 = (f16[784,768]{1,0:T(8,128)(2,1)}, f16[784,768]{1,0:T(8,128)(2,1)}, u32[]{:S(2)}, u32[]{:S(2)}) collective-permute-start(f16[784,768]{1,0:T(8,128)(2,1)} %get-tuple-element.30), channel_id=1, source_target_pairs={{0,64},{32,96},{64,0},{96,32},{1,65},{33,97},{65,1},{97,33},{2,66}... | collective-permute-start | bytes 3612680 | tf_op jit(solution)/shard_map/ppermute | solution.py:25
  8.4 8.7 %multiply_convert_fusion = f16[1024,768]{1,0:T(8,128)(2,1)S(1)} fusion(bf16[3072,1024]{1,0:T(8,128)(2,1)} %param.7, bf16[768,3072]{1,0:T(8,128)(2,1)S(1)} %copy-done.2), kind=kOutput, calls=%fused_computation.9 | convolution fusion | flops 4835770368 | bytes 12582912 | tf_op jit(solution)/shard_map/dot_general | solution.py:167
  17.1 1.6 %copy.7 = f16[4,16,2,8,6,128]{5,3,4,0,2,1:T(8,128)(2,1)} copy(f16[4,16,2,8,6,128]{5,3,4,2,1,0:T(8,128)(2,1)S(1)} %bitcast.39) | data formatting | bytes 3145728 | tf_op jit(solution)/shard_map/reshape | solution.py:171
  18.7 8.1 %all-to-all-start = ((f16[16,384,128]{2,1,0:T(8,128)(2,1)}), f16[16,384,128]{2,1,0:T(8,128)(2,1)}, u32[]{:S(2)}, u32[]{:S(2)}) async-start(f16[16,384,128]{2,1,0:T(8,128)(2,1)} %bitcast.33), calls=%async_computation | async-start | bytes 3145728 | tf_op jit(solution)/shard_map/all_to_all | solution.py:174
  26.8 1.7 %fusion.8 = (bf16[784,768]{1,0:T(8,128)(2,1)}, bf16[784,768]{1,0:T(8,128)(2,1)}) fusion(f32[784,768]{1,0:T(8,128)S(1)} %get-tuple-element.18), kind=kLoop, calls=%fused_computation.20 | loop fusion | flops 2408448 | bytes 4816896 | tf_op jit(solution)/shard_map/convert_element_type | solution.py:47
  29.1 6.9 %collective-permute-done.6 = f16[784,768]{1,0:T(8,128)(2,1)} collective-permute-done((f16[784,768]{1,0:T(8,128)(2,1)}, f16[784,768]{1,0:T(8,128)(2,1)}, u32[]{:S(2)}, u32[]{:S(2)}) %collective-permute-start.6) | collective-permute-done | bytes 1204256 | tf_op jit(solution)/shard_map/ppermute | solution.py:25
  36.0 1.9 %fusion.9 = (bf16[784,768]{1,0:T(8,128)(2,1)S(1)}, bf16[784,768]{1,0:T(8,128)(2,1)S(1)}) fusion(f16[784,768]{1,0:T(8,128)(2,1)} %collective-permute-done.6), kind=kLoop, calls=%fused_computation.21 | loop fusion | flops 4816896 | bytes 3612672 | tf_op jit(solution)/shard_map/convert_element_type | solution.py:47
  38.4 13.0 %all-to-all-done = f16[16,384,128]{2,1,0:T(8,128)(2,1)} async-done(((f16[16,384,128]{2,1,0:T(8,128)(2,1)}), f16[16,384,128]{2,1,0:T(8,128)(2,1)}, u32[]{:S(2)}, u32[]{:S(2)}) %all-to-all-start) | async-done | bytes 1572896 | tf_op jit(solution)/shard_map/all_to_all | solution.py:174
  51.4 1.9 %fusion.1 = f32[384,128]{1,0:T(8,128)S(1)} fusion(f16[16,384,128]{2,1,0:T(8,128)(2,1)} %all-to-all-done), kind=kLoop, calls=%fused_computation.7 | loop fusion | flops 3883008 | bytes 1769472 | tf_op jit(solution)/shard_map/reduce_sum | solution.py:181
  55.4 2.0 %collective-permute-start.3 = (f32[12,8,128]{2,1,0:T(8,128)S(1)}, f32[12,8,128]{2,1,0:T(8,128)S(1)}, u32[]{:S(2)}, u32[]{:S(2)}) collective-permute-start(f32[12,8,128]{2,1,0:T(8,128)S(1)} %get-tuple-element.36), channel_id=1, source_target_pairs={{0,64},{1,65},{2,66},{3,67},{4,68},{5,69},{6,70},{7,71},{8,72},{9,... | collective-permute-start | bytes 147464 | tf_op jit(solution)/shard_map/ppermute | solution.py:33
  57.5 2.1 %collective-permute-start.4 = (f32[12,8,128]{2,1,0:T(8,128)S(1)}, f32[12,8,128]{2,1,0:T(8,128)S(1)}, u32[]{:S(2)}, u32[]{:S(2)}) collective-permute-start(f32[12,8,128]{2,1,0:T(8,128)S(1)} %get-tuple-element.33), channel_id=1, source_target_pairs={{0,65},{1,64},{2,67},{3,66},{4,69},{5,68},{6,71},{7,70},{8,73},{9,... | collective-permute-start | bytes 147464 | tf_op jit(solution)/shard_map/ppermute | solution.py:33
  59.6 1.5 %collective-permute-done.3.far_ref = f32[12,8,128]{2,1,0:T(8,128)S(1)} collective-permute-done((f32[12,8,128]{2,1,0:T(8,128)S(1)}, f32[12,8,128]{2,1,0:T(8,128)S(1)}, u32[]{:S(2)}, u32[]{:S(2)}) %collective-permute-start.3) | collective-permute-done | bytes 49184 | tf_op jit(solution)/shard_map/ppermute | solution.py:33
  61.0 1.7 %collective-permute-done.4.both_ref = f32[12,8,128]{2,1,0:T(8,128)S(1)} collective-permute-done((f32[12,8,128]{2,1,0:T(8,128)S(1)}, f32[12,8,128]{2,1,0:T(8,128)S(1)}, u32[]{:S(2)}, u32[]{:S(2)}) %collective-permute-start.4) | collective-permute-done | bytes 49184 | tf_op jit(solution)/shard_map/ppermute | solution.py:33
  62.8 8.6 %iterate.1 = (bf16[32,12,8,128]{3,2,1,0:T(8,128)(2,1)}, bf16[12,8,128]{2,1,0:T(8,128)(2,1)S(1)}) custom-call(s32[24]{0:T(128)S(1)} %copy-done, s32[24]{0:T(128)S(1)} %copy-done.1, s32[1]{0:T(128)} %bitcast.me_ref, f32[12,8,128]{2,1,0:T(8,128)S(1)} %get-tuple-element.34.kept_ref, f32[12,8,128]{2,1,0:T(8,128)S(1)} %collective-permute-done.2.next_ref, ...), custom_call_target="tpu_custom_call" | custom-call | flops 1811939328 | bytes 9437184 | tf_op jit(solution)/shard_map/iterate/pallas_call | solution.py:202
  71.4 3.9 %all-to-all-start.2 = ((bf16[32,12,8,128]{3,2,1,0:T(8,128)(2,1)}), bf16[32,12,8,128]{3,2,1,0:T(8,128)(2,1)S(1)}, u32[]{:S(2)}, u32[]{:S(2)}) async-start(bf16[32,12,8,128]{3,2,1,0:T(8,128)(2,1)} %get-tuple-element.22), calls=%async_computation.2 | async-start | bytes 1572864 | tf_op jit(solution)/shard_map/all_to_all | solution.py:255
  75.4 3.1 %collective-permute-start.10 = (bf16[12,8,128]{2,1,0:T(8,128)(2,1)S(1)}, bf16[12,8,128]{2,1,0:T(8,128)(2,1)S(1)}, u32[]{:S(2)}, u32[]{:S(2)}) collective-permute-start(bf16[12,8,128]{2,1,0:T(8,128)(2,1)S(1)} %get-tuple-element.19), channel_id=1, source_target_pairs={{0,64},{1,65},{2,66},{3,67},{4,68},{5,69},{6,70},{7,71},{8,72},{9,... | collective-permute-start | bytes 73736 | tf_op jit(solution)/shard_map/ppermute | solution.py:33
  78.4 1.5 %collective-permute-start.11 = (bf16[12,8,128]{2,1,0:T(8,128)(2,1)S(1)}, bf16[12,8,128]{2,1,0:T(8,128)(2,1)S(1)}, u32[]{:S(2)}, u32[]{:S(2)}) collective-permute-start(bf16[12,8,128]{2,1,0:T(8,128)(2,1)S(1)} %get-tuple-element.19), channel_id=1, source_target_pairs={{0,65},{1,64},{2,67},{3,66},{4,69},{5,68},{6,71},{7,70},{8,73},{9,... | collective-permute-start | bytes 73736 | tf_op jit(solution)/shard_map/ppermute | solution.py:33
  79.9 6.4 %collective-permute-done.10 = bf16[12,8,128]{2,1,0:T(8,128)(2,1)S(1)} collective-permute-done((bf16[12,8,128]{2,1,0:T(8,128)(2,1)S(1)}, bf16[12,8,128]{2,1,0:T(8,128)(2,1)S(1)}, u32[]{:S(2)}, u32[]{:S(2)}) %collective-permute-start.10) | collective-permute-done | bytes 24608 | tf_op jit(solution)/shard_map/ppermute | solution.py:33
  86.3 3.4 %all-to-all-done.2 = bf16[32,12,8,128]{3,2,1,0:T(8,128)(2,1)S(1)} async-done(((bf16[32,12,8,128]{3,2,1,0:T(8,128)(2,1)}), bf16[32,12,8,128]{3,2,1,0:T(8,128)(2,1)S(1)}, u32[]{:S(2)}, u32[]{:S(2)}) %all-to-all-start.2) | async-done | bytes 786464 | tf_op jit(solution)/shard_map/all_to_all | solution.py:255
  90.7 3.7 %all-to-all-start.1 = ((bf16[16,2,12,8,128]{4,3,2,1,0:T(8,128)(2,1)}), bf16[16,2,12,8,128]{4,3,2,1,0:T(8,128)(2,1)S(1)}, u32[]{:S(2)}, u32[]{:S(2)}) async-start(bf16[16,2,12,8,128]{4,3,2,1,0:T(8,128)(2,1)} %broadcast_in_dim.23), calls=%async_computation.1 | async-start | bytes 1572864 | tf_op jit(solution)/shard_map/all_to_all | solution.py:57
  94.5 2.6 %fusion.19 = f32[256,1536]{1,0:T(8,128)S(1)} fusion(bf16[768,3072]{1,0:T(8,128)(2,1)} %param.6, bf16[256,1536]{1,0:T(8,128)(2,1)S(1)} %bitcast.41), kind=kOutput, calls=%fused_computation.33 | convolution fusion | flops 603979776 | bytes 4325376 | tf_op jit(solution)/shard_map/dot_general | solution.py:249
  97.1 3.4 %fusion.6 = bf16[256,1536]{1,0:T(8,128)(2,1)} fusion(f32[256,1536]{1,0:T(8,128)S(1)} %fusion.19, bf16[768,3072]{1,0:T(8,128)(2,1)} %collective-permute-done, bf16[256,1536]{1,0:T(8,128)(2,1)S(1)} %bitcast.42), kind=kOutput, calls=%fused_computation.18 | convolution fusion | flops 605159424 | bytes 5111808 | tf_op jit(solution)/shard_map/dot_general | solution.py:250
  100.4 2.6 %collective-permute-start.12 = (bf16[256,1536]{1,0:T(8,128)(2,1)}, bf16[256,1536]{1,0:T(8,128)(2,1)S(1)}, u32[]{:S(2)}, u32[]{:S(2)}) collective-permute-start(bf16[256,1536]{1,0:T(8,128)(2,1)} %fusion.6), channel_id=1, source_target_pairs={{0,64},{32,96},{64,0},{96,32},{1,65},{33,97},{65,1},{97,33},{2,66}... | collective-permute-start | bytes 2359304 | tf_op jit(solution)/shard_map/ppermute | solution.py:25
  103.8 2.5 %fusion.7 = bf16[256,1536]{1,0:T(8,128)(2,1)S(1)} fusion(f32[256,1536]{1,0:T(8,128)S(1)} %fusion.13, bf16[768,3072]{1,0:T(8,128)(2,1)} %collective-permute-done, bf16[256,1536]{1,0:T(8,128)(2,1)S(1)} %bitcast.44), kind=kOutput, calls=%fused_computation.19 | convolution fusion | flops 605159424 | bytes 5111808 | tf_op jit(solution)/shard_map/dot_general | solution.py:250
  107.3 2.4 %fusion.15 = f32[256,1536]{1,0:T(8,128)S(1)} fusion(bf16[768,3072]{1,0:T(8,128)(2,1)} %param.6, bf16[256,1536]{1,0:T(8,128)(2,1)S(1)} %bitcast.34), kind=kOutput, calls=%fused_computation.29 | convolution fusion | flops 603979776 | bytes 4325376 | tf_op jit(solution)/shard_map/dot_general | solution.py:249
  109.8 2.4 %fusion.21 = f32[256,1536]{1,0:T(8,128)S(1)} fusion(bf16[768,3072]{1,0:T(8,128)(2,1)} %param.6, bf16[256,1536]{1,0:T(8,128)(2,1)S(1)} %bitcast.35), kind=kOutput, calls=%fused_computation.35 | convolution fusion | flops 603979776 | bytes 4325376 | tf_op jit(solution)/shard_map/dot_general | solution.py:249
  112.2 2.5 %fusion.4 = f32[256,1536]{1,0:T(8,128)S(1)} fusion(f32[256,1536]{1,0:T(8,128)S(1)} %fusion.15, bf16[768,3072]{1,0:T(8,128)(2,1)} %collective-permute-done, bf16[256,1536]{1,0:T(8,128)(2,1)S(1)} %bitcast.36), kind=kOutput, calls=%fused_computation.15 | convolution fusion | flops 604766208 | bytes 5898240 | tf_op jit(solution)/shard_map/dot_general | solution.py:250
  114.7 2.5 %fusion.5 = f32[256,1536]{1,0:T(8,128)S(1)} fusion(f32[256,1536]{1,0:T(8,128)S(1)} %fusion.21, bf16[768,3072]{1,0:T(8,128)(2,1)} %collective-permute-done, bf16[256,1536]{1,0:T(8,128)(2,1)S(1)} %bitcast.37), kind=kOutput, calls=%fused_computation.17 | convolution fusion | flops 604766208 | bytes 5898240 | tf_op jit(solution)/shard_map/dot_general | solution.py:250
  117.2 5.4 %collective-permute-done.12 = bf16[256,1536]{1,0:T(8,128)(2,1)S(1)} collective-permute-done((bf16[256,1536]{1,0:T(8,128)(2,1)}, bf16[256,1536]{1,0:T(8,128)(2,1)S(1)}, u32[]{:S(2)}, u32[]{:S(2)}) %collective-permute-start.12) | collective-permute-done | bytes 786464 | tf_op jit(solution)/shard_map/ppermute | solution.py:25
  122.8 13.3 %collective-permute-done.13 = bf16[256,1536]{1,0:T(8,128)(2,1)} collective-permute-done((bf16[256,1536]{1,0:T(8,128)(2,1)S(1)}, bf16[256,1536]{1,0:T(8,128)(2,1)}, u32[]{:S(2)}, u32[]{:S(2)}) %collective-permute-start.13) | collective-permute-done | bytes 786464 | tf_op jit(solution)/shard_map/ppermute | solution.py:25
  137.4 1.9 %pad_maximum_fusion = f32[256,3072]{1,0:T(8,128)} fusion(f32[256,1536]{1,0:T(8,128)S(1)} %convert_add_fusion, f32[256,1536]{1,0:T(8,128)S(1)} %convert_add_fusion.1), kind=kLoop, calls=%fused_computation.8 | loop fusion | flops 786432 | bytes 6291456 | tf_op jit(solution)/shard_map/concatenate | solution.py:265
  (39 shorter events, 8.4 us)
Async XLA Ops:
  0.0 51.4 %collective-permute-start = (bf16[768,3072]{1,0:T(8,128)(2,1)}, bf16[768,3072]{1,0:T(8,128)(2,1)}, u32[]{:S(2)}, u32[]{:S(2)}) collective-permute-start(bf16[768,3072]{1,0:T(8,128)(2,1)} %param.6), channel_id=1, source_target_pairs={{0,32},{32,0},{64,96},{96,64},{1,33},{33,1},{65,97},{97,65},{2,34}... | collective-permute-start | bytes 14155784 | tf_op jit(solution)/shard_map/ppermute | solution.py:25
  0.8 7.6 %copy-start.2 = (bf16[768,3072]{1,0:T(8,128)(2,1)S(1)}, bf16[768,3072]{1,0:T(8,128)(2,1)}, u32[]{:S(2)}) copy-start(bf16[768,3072]{1,0:T(8,128)(2,1)} %param.6) | copy-start | bytes 14155780
  5.3 30.7 %collective-permute-start.6 = (f16[784,768]{1,0:T(8,128)(2,1)}, f16[784,768]{1,0:T(8,128)(2,1)}, u32[]{:S(2)}, u32[]{:S(2)}) collective-permute-start(f16[784,768]{1,0:T(8,128)(2,1)} %get-tuple-element.30), channel_id=1, source_target_pairs={{0,64},{32,96},{64,0},{96,32},{1,65},{33,97},{65,1},{97,33},{2,66}... | collective-permute-start | bytes 3612680 | tf_op jit(solution)/shard_map/ppermute | solution.py:25
  18.7 32.7 %all-to-all-start = ((f16[16,384,128]{2,1,0:T(8,128)(2,1)}), f16[16,384,128]{2,1,0:T(8,128)(2,1)}, u32[]{:S(2)}, u32[]{:S(2)}) async-start(f16[16,384,128]{2,1,0:T(8,128)(2,1)} %bitcast.33), calls=%async_computation | async-start | bytes 3145728 | tf_op jit(solution)/shard_map/all_to_all | solution.py:174
  28.6 26.9 %collective-permute-start.5 = (bf16[784,768]{1,0:T(8,128)(2,1)}, bf16[784,768]{1,0:T(8,128)(2,1)}, u32[]{:S(2)}, u32[]{:S(2)}) collective-permute-start(bf16[784,768]{1,0:T(8,128)(2,1)} %get-tuple-element.28.refs_0_), channel_id=1, source_target_pairs={{0,32},{32,0},{64,96},{96,64},{1,33},{33,1},{65,97},{97,65},{2,34}... | collective-permute-start | bytes 3612680 | tf_op jit(solution)/shard_map/ppermute | solution.py:25
  28.6 34.2 %copy-start = (s32[24]{0:T(128)S(1)}, s32[24]{0:T(128)}, u32[]{:S(2)}) copy-start(s32[24]{0:T(128)} %owner_ref.1) | copy-start | bytes 292
  28.6 34.2 %copy-start.1 = (s32[24]{0:T(128)S(1)}, s32[24]{0:T(128)}, u32[]{:S(2)}) copy-start(s32[24]{0:T(128)} %live_ref.1) | copy-start | bytes 292
  28.6 28.9 %collective-permute-start.8 = (bf16[784,768]{1,0:T(8,128)(2,1)}, bf16[784,768]{1,0:T(8,128)(2,1)}, u32[]{:S(2)}, u32[]{:S(2)}) collective-permute-start(bf16[784,768]{1,0:T(8,128)(2,1)} %get-tuple-element.27.refs_4_), channel_id=1, source_target_pairs={{0,32},{32,0},{64,96},{96,64},{1,33},{33,1},{65,97},{97,65},{2,34}... | collective-permute-start | bytes 3612680 | tf_op jit(solution)/shard_map/ppermute | solution.py:25
  37.8 21.7 %collective-permute-start.7 = (bf16[784,768]{1,0:T(8,128)(2,1)S(1)}, bf16[784,768]{1,0:T(8,128)(2,1)}, u32[]{:S(2)}, u32[]{:S(2)}) collective-permute-start(bf16[784,768]{1,0:T(8,128)(2,1)S(1)} %get-tuple-element.32.refs_2_), channel_id=1, source_target_pairs={{0,32},{32,0},{64,96},{96,64},{1,33},{33,1},{65,97},{97,65},{2,34}... | collective-permute-start | bytes 3612680 | tf_op jit(solution)/shard_map/ppermute | solution.py:25
  37.9 21.6 %collective-permute-start.9 = (bf16[784,768]{1,0:T(8,128)(2,1)S(1)}, bf16[784,768]{1,0:T(8,128)(2,1)}, u32[]{:S(2)}, u32[]{:S(2)}) collective-permute-start(bf16[784,768]{1,0:T(8,128)(2,1)S(1)} %get-tuple-element.31.refs_6_), channel_id=1, source_target_pairs={{0,32},{32,0},{64,96},{96,64},{1,33},{33,1},{65,97},{97,65},{2,34}... | collective-permute-start | bytes 3612680 | tf_op jit(solution)/shard_map/ppermute | solution.py:25
  53.4 1.4 collective-permute-start.1
  54.8 4.8 %collective-permute-start.2 = (f32[12,8,128]{2,1,0:T(8,128)S(1)}, f32[12,8,128]{2,1,0:T(8,128)S(1)}, u32[]{:S(2)}, u32[]{:S(2)}) collective-permute-start(f32[12,8,128]{2,1,0:T(8,128)S(1)} %get-tuple-element.35), channel_id=1, source_target_pairs={{0,1},{1,0},{2,3},{3,2},{4,5},{5,4},{6,7},{7,6},{8,9},{9,8},{10,11... | collective-permute-start | bytes 147464 | tf_op jit(solution)/shard_map/ppermute | solution.py:33
  55.4 5.6 %collective-permute-start.3 = (f32[12,8,128]{2,1,0:T(8,128)S(1)}, f32[12,8,128]{2,1,0:T(8,128)S(1)}, u32[]{:S(2)}, u32[]{:S(2)}) collective-permute-start(f32[12,8,128]{2,1,0:T(8,128)S(1)} %get-tuple-element.36), channel_id=1, source_target_pairs={{0,64},{1,65},{2,66},{3,67},{4,68},{5,69},{6,70},{7,71},{8,72},{9,... | collective-permute-start | bytes 147464 | tf_op jit(solution)/shard_map/ppermute | solution.py:33
  57.5 5.3 %collective-permute-start.4 = (f32[12,8,128]{2,1,0:T(8,128)S(1)}, f32[12,8,128]{2,1,0:T(8,128)S(1)}, u32[]{:S(2)}, u32[]{:S(2)}) collective-permute-start(f32[12,8,128]{2,1,0:T(8,128)S(1)} %get-tuple-element.33), channel_id=1, source_target_pairs={{0,65},{1,64},{2,67},{3,66},{4,69},{5,68},{6,71},{7,70},{8,73},{9,... | collective-permute-start | bytes 147464 | tf_op jit(solution)/shard_map/ppermute | solution.py:33
  71.4 18.3 %all-to-all-start.2 = ((bf16[32,12,8,128]{3,2,1,0:T(8,128)(2,1)}), bf16[32,12,8,128]{3,2,1,0:T(8,128)(2,1)S(1)}, u32[]{:S(2)}, u32[]{:S(2)}) async-start(bf16[32,12,8,128]{3,2,1,0:T(8,128)(2,1)} %get-tuple-element.22), calls=%async_computation.2 | async-start | bytes 1572864 | tf_op jit(solution)/shard_map/all_to_all | solution.py:255
  75.4 10.9 %collective-permute-start.10 = (bf16[12,8,128]{2,1,0:T(8,128)(2,1)S(1)}, bf16[12,8,128]{2,1,0:T(8,128)(2,1)S(1)}, u32[]{:S(2)}, u32[]{:S(2)}) collective-permute-start(bf16[12,8,128]{2,1,0:T(8,128)(2,1)S(1)} %get-tuple-element.19), channel_id=1, source_target_pairs={{0,64},{1,65},{2,66},{3,67},{4,68},{5,69},{6,70},{7,71},{8,72},{9,... | collective-permute-start | bytes 73736 | tf_op jit(solution)/shard_map/ppermute | solution.py:33
  78.4 7.9 %collective-permute-start.11 = (bf16[12,8,128]{2,1,0:T(8,128)(2,1)S(1)}, bf16[12,8,128]{2,1,0:T(8,128)(2,1)S(1)}, u32[]{:S(2)}, u32[]{:S(2)}) collective-permute-start(bf16[12,8,128]{2,1,0:T(8,128)(2,1)S(1)} %get-tuple-element.19), channel_id=1, source_target_pairs={{0,65},{1,64},{2,67},{3,66},{4,69},{5,68},{6,71},{7,70},{8,73},{9,... | collective-permute-start | bytes 73736 | tf_op jit(solution)/shard_map/ppermute | solution.py:33
  90.7 12.3 %slice-start = ((s8[4718592]{0:T(1024)(128)(4,1)}), s8[524288]{0:T(1024)(128)(4,1)S(1)}, s32[]{:S(2)}) async-start(s8[4718592]{0:T(1024)(128)(4,1)} %bitcast.47), calls=%async_computation.3 | async-start | bytes 1048576
  90.7 16.6 %all-to-all-start.1 = ((bf16[16,2,12,8,128]{4,3,2,1,0:T(8,128)(2,1)}), bf16[16,2,12,8,128]{4,3,2,1,0:T(8,128)(2,1)S(1)}, u32[]{:S(2)}, u32[]{:S(2)}) async-start(bf16[16,2,12,8,128]{4,3,2,1,0:T(8,128)(2,1)} %broadcast_in_dim.23), calls=%async_computation.1 | async-start | bytes 1572864 | tf_op jit(solution)/shard_map/all_to_all | solution.py:57
  94.5 8.5 %slice-start.1 = ((s8[4718592]{0:T(1024)(128)(4,1)}), s8[4194304]{0:T(1024)(128)(4,1)S(1)}, s32[]{:S(2)}) async-start(s8[4718592]{0:T(1024)(128)(4,1)} %bitcast.47), calls=%async_computation.4 | async-start | bytes 8388608
  100.4 22.1 %collective-permute-start.12 = (bf16[256,1536]{1,0:T(8,128)(2,1)}, bf16[256,1536]{1,0:T(8,128)(2,1)S(1)}, u32[]{:S(2)}, u32[]{:S(2)}) collective-permute-start(bf16[256,1536]{1,0:T(8,128)(2,1)} %fusion.6), channel_id=1, source_target_pairs={{0,64},{32,96},{64,0},{96,32},{1,65},{33,97},{65,1},{97,33},{2,66}... | collective-permute-start | bytes 2359304 | tf_op jit(solution)/shard_map/ppermute | solution.py:25
  106.3 29.8 %collective-permute-start.13 = (bf16[256,1536]{1,0:T(8,128)(2,1)S(1)}, bf16[256,1536]{1,0:T(8,128)(2,1)}, u32[]{:S(2)}, u32[]{:S(2)}) collective-permute-start(bf16[256,1536]{1,0:T(8,128)(2,1)S(1)} %fusion.7), channel_id=1, source_target_pairs={{0,64},{32,96},{64,0},{96,32},{1,65},{33,97},{65,1},{97,33},{2,66}... | collective-permute-start | bytes 2359304 | tf_op jit(solution)/shard_map/ppermute | solution.py:25

commit v2 on v1

--- a/solution.py
+++ b/solution.py
@@ -13,11 +13,10 @@
 DAMPING = 0.6
 COUPLING = 0.5
 PAD = 8
-CHUNKS = 2
+FIRST = 3
 LISTED = 16.0
 MIB = 1 << 20
 PART_SCALE = 2048.0
-FLEX_SCALE = 131072.0
 
 
 def swap(array, flip):
@@ -84,7 +83,8 @@
     places = [me ^ flip for flip in range(4)]
 
     def place_of(block):
-        return ((block // count) ^ me) * count + lax.rem(block, count)
+        row = sum((block >= k * count).astype(jnp.int32) for k in range(1, 4))
+        return block + ((row ^ me) - row) * count
 
     for b in range(total):
         inverse_ref[owner_ref[b]] = b
@@ -159,7 +159,7 @@
     flex_own = jnp.concatenate(
         [flex_own, jnp.broadcast_to(lists[:, None], (2 * PAD, order_rows))], axis=0
     )
-    flex_packed = to_root(flex_own, FLEX_SCALE)
+    flex_packed = (flex_own * 262144.0).astype(jnp.float16)
     flex_far = swap(flex_packed, 2)
     panel_beside = swap(panel, 1)
     surface, flex_packed, flex_own = lax.optimization_barrier((surface, flex_packed, flex_own))
@@ -172,13 +172,13 @@
     pieces = pieces.transpose(1, 2, 0, 4, 3, 5)
     pieces = pieces.reshape(col_total // 2, 2 * row_total * block_count * group, MBLK)
     received = lax.all_to_all(pieces, "col", 0, 0, axis_index_groups=planes(), tiled=True)
-    received, panel_beside = lax.optimization_barrier((received, panel_beside))
 
     high, low = split_in_two(flex_own)
-    far_high, far_low = split_in_two(from_root(flex_far, FLEX_SCALE))
+    far_high, far_low = split_in_two((flex_far.astype(jnp.float32) / 262144.0))
     highs = [high, swap(high, 1), far_high, swap(far_high, 1)]
     lows = [low, swap(low, 1), far_low, swap(far_low, 1)]
     traction = jnp.sum(from_root(received, PART_SCALE), axis=0)
+    traction, panel_beside = lax.optimization_barrier((traction, panel_beside))
 
     own_far = own_row // 2
     own_core = own_row % 2
@@ -241,8 +241,8 @@
         values = everyones.reshape(col_total, 2 * block_count, group, MBLK).transpose(0, 2, 1, 3)
         return values.reshape(col_total * group, 2 * order_rows)
 
-    width = column_count // CHUNKS
-    cuts = [slice(i * width, (i + 1) * width) for i in range(CHUNKS)]
+    first = column_count // FIRST
+    cuts = [slice(0, first), slice(first, column_count)]
 
     def times_panel(values, cut):
         return gain_factor * (

time: 140 us -> 136 us (0.971)
  the two profiles are of different devices: /device:TPU:0 before, /device:TPU:1 now
where the time goes in v2:
time: 136 us; the launch traced here: 134 us
  waiting for transfers between devices  46.9 us (34%)
  starting transfers between devices  34.1 us (25%)
  matrix products  30.1 us (22%)
  other arithmetic  11.7 us (9%)
  Pallas kernels  8.62 us (6%)
  local copies, waits for them, and re-layouts  2.87 us (2%)
    ppermute x9, waiting for transfers between devices, swap(): return lax.ppermute(array, 'row', [(i, i ^ flip) for i in range(rows)])  23.4 us
    dot_general x4, matrix products, times_panel(): jnp.dot(values[:, order_rows:], panel_beside[:, cut], preferred_element_t...  11.6 us
    ppermute x9, starting transfers between devices, swap(): return lax.ppermute(array, 'row', [(i, i ^ flip) for i in range(rows)])  11.3 us
    all_to_all x1, waiting for transfers between devices, body(): lax.all_to_all(pieces, 'col', 0, 0, axis_index_groups=planes(), tiled=True)  11.2 us
    dot_general x4, matrix products, times_panel(): jnp.dot(values[:, :order_rows], panel[:, cut], preferred_element_type=jnp...  9.69 us
    ppermute x5, waiting for transfers between devices, far_swap(): return lax.ppermute(array, ('row', 'col'), pairs)  9.04 us
    dot_general x1, matrix products, body(): lax.dot_general(surface, panel, (((0,), (1,)), ((), ())), preferred_eleme...  8.74 us
    pallas_call x1, Pallas kernels, body(): pl.pallas_call(iterate, out_shape=(jax.ShapeDtypeStruct((col_total, *shap...  8.62 us
  transfers between devices with their start and end apart: 17, of which 9 were waited for; matrix products, arithmetic and copies ran while one was open for 31% of the time, Pallas kernels for 0%

profile of v2, /device:TPU:1, one launch (start us, length us, event | category | flops | bytes accessed | tf_op | source)
XLA Modules:
  0.0 134.4 jit_solution(6515286237712836222)
XLA Ops:
  0.0 1.4 %collective-permute-start = (bf16[768,3072]{1,0:T(8,128)(2,1)}, bf16[768,3072]{1,0:T(8,128)(2,1)}, u32[]{:S(2)}, u32[]{:S(2)}) collective-permute-start(bf16[768,3072]{1,0:T(8,128)(2,1)} %param.6), channel_id=1, source_target_pairs={{0,32},{32,0},{64,96},{96,64},{1,33},{33,1},{65,97},{97,65},{2,34}... | collective-permute-start | bytes 14155784 | tf_op jit(solution)/shard_map/ppermute | solution.py:24
  2.2 3.2 %pad_maximum_fusion.1 = (f32[784,768]{1,0:T(8,128)S(1)}, f16[784,768]{1,0:T(8,128)(2,1)}) fusion(f32[768,768]{1,0:T(8,128)} %bitcast.38, f32[784]{0:T(1024)S(1)} %pad.9.clone), kind=kLoop, calls=%fused_computation.24 | loop fusion | flops 1806336 | bytes 5975104 | tf_op jit(solution)/shard_map/concatenate | solution.py:159
  5.4 2.9 %collective-permute-start.6 = (f16[784,768]{1,0:T(8,128)(2,1)}, f16[784,768]{1,0:T(8,128)(2,1)}, u32[]{:S(2)}, u32[]{:S(2)}) collective-permute-start(f16[784,768]{1,0:T(8,128)(2,1)} %get-tuple-element.30), channel_id=1, source_target_pairs={{0,64},{32,96},{64,0},{96,32},{1,65},{33,97},{65,1},{97,33},{2,66}... | collective-permute-start | bytes 3612680 | tf_op jit(solution)/shard_map/ppermute | solution.py:24
  8.3 8.7 %multiply_convert_fusion = f16[1024,768]{1,0:T(8,128)(2,1)S(1)} fusion(bf16[3072,1024]{1,0:T(8,128)(2,1)} %param.7, bf16[768,3072]{1,0:T(8,128)(2,1)S(1)} %copy-done.2), kind=kOutput, calls=%fused_computation.8 | convolution fusion | flops 4835770368 | bytes 12582912 | tf_op jit(solution)/shard_map/dot_general | solution.py:167
  17.0 1.6 %copy.7 = f16[4,16,2,8,6,128]{5,3,4,0,2,1:T(8,128)(2,1)} copy(f16[4,16,2,8,6,128]{5,3,4,2,1,0:T(8,128)(2,1)S(1)} %bitcast.39) | data formatting | bytes 3145728 | tf_op jit(solution)/shard_map/reshape | solution.py:171
  18.6 7.8 %all-to-all-start = ((f16[16,384,128]{2,1,0:T(8,128)(2,1)}), f16[16,384,128]{2,1,0:T(8,128)(2,1)}, u32[]{:S(2)}, u32[]{:S(2)}) async-start(f16[16,384,128]{2,1,0:T(8,128)(2,1)} %bitcast.33), calls=%async_computation | async-start | bytes 3145728 | tf_op jit(solution)/shard_map/all_to_all | solution.py:174
  26.4 1.8 %fusion.25 = (bf16[784,768]{1,0:T(8,128)(2,1)}, bf16[784,768]{1,0:T(8,128)(2,1)}) fusion(f32[784,768]{1,0:T(8,128)S(1)} %get-tuple-element.18), kind=kLoop, calls=%fused_computation.22 | loop fusion | flops 2408448 | bytes 4816896 | tf_op jit(solution)/shard_map/convert_element_type | solution.py:46
  28.9 6.4 %collective-permute-done.6 = f16[784,768]{1,0:T(8,128)(2,1)} collective-permute-done((f16[784,768]{1,0:T(8,128)(2,1)}, f16[784,768]{1,0:T(8,128)(2,1)}, u32[]{:S(2)}, u32[]{:S(2)}) %collective-permute-start.6) | collective-permute-done | bytes 1204256 | tf_op jit(solution)/shard_map/ppermute | solution.py:24
  35.3 1.7 %fusion.26 = (bf16[784,768]{1,0:T(8,128)(2,1)S(1)}, bf16[784,768]{1,0:T(8,128)(2,1)S(1)}) fusion(f16[784,768]{1,0:T(8,128)(2,1)} %collective-permute-done.6), kind=kLoop, calls=%fused_computation.23 | loop fusion | flops 3612672 | bytes 3612672 | tf_op jit(solution)/shard_map/convert_element_type | solution.py:46
  38.0 11.2 %all-to-all-done = f16[16,384,128]{2,1,0:T(8,128)(2,1)} async-done(((f16[16,384,128]{2,1,0:T(8,128)(2,1)}), f16[16,384,128]{2,1,0:T(8,128)(2,1)}, u32[]{:S(2)}, u32[]{:S(2)}) %all-to-all-start) | async-done | bytes 1572896 | tf_op jit(solution)/shard_map/all_to_all | solution.py:174
  49.2 1.9 %fusion.1 = f32[384,128]{1,0:T(8,128)S(1)} fusion(f16[16,384,128]{2,1,0:T(8,128)(2,1)} %all-to-all-done), kind=kLoop, calls=%fused_computation.6 | loop fusion | flops 3883008 | bytes 1769472 | tf_op jit(solution)/shard_map/reduce_sum | solution.py:180
  51.2 2.4 %collective-permute-start.1 = (f32[4,6,8,128]{3,2,1,0:T(8,128)S(1)}, f32[4,6,8,128]{3,2,1,0:T(8,128)S(1)}, u32[]{:S(2)}, u32[]{:S(2)}) collective-permute-start(f32[4,6,8,128]{3,2,1,0:T(8,128)S(1)} %get-tuple-element.37), channel_id=1, source_target_pairs={{0,32},{32,0},{64,96},{96,64},{1,33},{33,1},{65,97},{97,65},{2,34}... | collective-permute-start | bytes 294920 | tf_op jit(solution)/shard_map/ppermute | solution.py:24
  55.5 3.0 %collective-permute-start.3 = (f32[12,8,128]{2,1,0:T(8,128)S(1)}, f32[12,8,128]{2,1,0:T(8,128)S(1)}, u32[]{:S(2)}, u32[]{:S(2)}) collective-permute-start(f32[12,8,128]{2,1,0:T(8,128)S(1)} %get-tuple-element.36), channel_id=1, source_target_pairs={{0,64},{1,65},{2,66},{3,67},{4,68},{5,69},{6,70},{7,71},{8,72},{9,... | collective-permute-start | bytes 147464 | tf_op jit(solution)/shard_map/ppermute | solution.py:32
  58.8 1.7 %collective-permute-done.3.far_ref = f32[12,8,128]{2,1,0:T(8,128)S(1)} collective-permute-done((f32[12,8,128]{2,1,0:T(8,128)S(1)}, f32[12,8,128]{2,1,0:T(8,128)S(1)}, u32[]{:S(2)}, u32[]{:S(2)}) %collective-permute-start.3) | collective-permute-done | bytes 49184 | tf_op jit(solution)/shard_map/ppermute | solution.py:32
  60.5 8.6 %iterate.1 = (bf16[32,12,8,128]{3,2,1,0:T(8,128)(2,1)}, bf16[12,8,128]{2,1,0:T(8,128)(2,1)S(1)}) custom-call(s32[24]{0:T(128)S(1)} %copy-done, s32[24]{0:T(128)S(1)} %copy-done.1, s32[1]{0:T(128)} %bitcast.me_ref, f32[12,8,128]{2,1,0:T(8,128)S(1)} %get-tuple-element.34.kept_ref, f32[12,8,128]{2,1,0:T(8,128)S(1)} %collective-permute-done.2.next_ref, ...), custom_call_target="tpu_custom_call" | custom-call | flops 1811939328 | bytes 9437184 | tf_op jit(solution)/shard_map/iterate/pallas_call | solution.py:202
  69.1 4.3 %all-to-all-start.2 = ((bf16[32,12,8,128]{3,2,1,0:T(8,128)(2,1)}), bf16[32,12,8,128]{3,2,1,0:T(8,128)(2,1)S(1)}, u32[]{:S(2)}, u32[]{:S(2)}) async-start(bf16[32,12,8,128]{3,2,1,0:T(8,128)(2,1)} %get-tuple-element.22), calls=%async_computation.2 | async-start | bytes 1572864 | tf_op jit(solution)/shard_map/all_to_all | solution.py:255
  73.5 2.2 %collective-permute-start.11 = (bf16[12,8,128]{2,1,0:T(8,128)(2,1)S(1)}, bf16[12,8,128]{2,1,0:T(8,128)(2,1)S(1)}, u32[]{:S(2)}, u32[]{:S(2)}) collective-permute-start(bf16[12,8,128]{2,1,0:T(8,128)(2,1)S(1)} %get-tuple-element.19), channel_id=1, source_target_pairs={{0,65},{1,64},{2,67},{3,66},{4,69},{5,68},{6,71},{7,70},{8,73},{9,... | collective-permute-start | bytes 73736 | tf_op jit(solution)/shard_map/ppermute | solution.py:32
  77.4 6.2 %collective-permute-done.10 = bf16[12,8,128]{2,1,0:T(8,128)(2,1)S(1)} collective-permute-done((bf16[12,8,128]{2,1,0:T(8,128)(2,1)S(1)}, bf16[12,8,128]{2,1,0:T(8,128)(2,1)S(1)}, u32[]{:S(2)}, u32[]{:S(2)}) %collective-permute-start.10) | collective-permute-done | bytes 24608 | tf_op jit(solution)/shard_map/ppermute | solution.py:32
  83.6 3.3 %all-to-all-done.2 = bf16[32,12,8,128]{3,2,1,0:T(8,128)(2,1)S(1)} async-done(((bf16[32,12,8,128]{3,2,1,0:T(8,128)(2,1)}), bf16[32,12,8,128]{3,2,1,0:T(8,128)(2,1)S(1)}, u32[]{:S(2)}, u32[]{:S(2)}) %all-to-all-start.2) | async-done | bytes 786464 | tf_op jit(solution)/shard_map/all_to_all | solution.py:255
  86.9 1.1 broadcast_in_dim.23
  88.0 3.6 %all-to-all-start.1 = ((bf16[16,2,12,8,128]{4,3,2,1,0:T(8,128)(2,1)}), bf16[16,2,12,8,128]{4,3,2,1,0:T(8,128)(2,1)S(1)}, u32[]{:S(2)}, u32[]{:S(2)}) async-start(bf16[16,2,12,8,128]{4,3,2,1,0:T(8,128)(2,1)} %broadcast_in_dim.23), calls=%async_computation.1 | async-start | bytes 1572864 | tf_op jit(solution)/shard_map/all_to_all | solution.py:56
  91.6 2.0 %fusion.31 = f32[256,1024]{1,0:T(8,128)S(1)} fusion(bf16[768,3072]{1,0:T(8,128)(2,1)} %param.6, bf16[256,1536]{1,0:T(8,128)(2,1)S(1)} %bitcast.41), kind=kOutput, calls=%fused_computation.32 | convolution fusion | flops 402653184 | bytes 3014656 | tf_op jit(solution)/shard_map/dot_general | solution.py:249
  93.6 2.8 %fusion.47 = bf16[256,1024]{1,0:T(8,128)(2,1)} fusion(f32[256,1024]{1,0:T(8,128)S(1)} %fusion.31, bf16[768,3072]{1,0:T(8,128)(2,1)} %collective-permute-done, bf16[256,1536]{1,0:T(8,128)(2,1)S(1)} %bitcast.42), kind=kOutput, calls=%fused_computation.40 | convolution fusion | flops 403439616 | bytes 3538944 | tf_op jit(solution)/shard_map/dot_general | solution.py:250
  96.4 2.1 %collective-permute-start.12 = (bf16[256,1024]{1,0:T(8,128)(2,1)}, bf16[256,1024]{1,0:T(8,128)(2,1)S(1)}, u32[]{:S(2)}, u32[]{:S(2)}) collective-permute-start(bf16[256,1024]{1,0:T(8,128)(2,1)} %fusion.47), channel_id=1, source_target_pairs={{0,64},{32,96},{64,0},{96,32},{1,65},{33,97},{65,1},{97,33},{2,66}... | collective-permute-start | bytes 1572872 | tf_op jit(solution)/shard_map/ppermute | solution.py:24
  98.5 2.9 %fusion.6 = f32[256,2048]{1,0:T(8,128)S(1)} fusion(bf16[768,3072]{1,0:T(8,128)(2,1)} %param.6, bf16[256,1536]{1,0:T(8,128)(2,1)S(1)} %bitcast.43), kind=kOutput, calls=%fused_computation.13 | convolution fusion | flops 805306368 | bytes 5636096 | tf_op jit(solution)/shard_map/dot_general | solution.py:249
  101.4 3.9 %fusion.22 = bf16[256,2048]{1,0:T(8,128)(2,1)} fusion(f32[256,2048]{1,0:T(8,128)S(1)} %fusion.6, bf16[768,3072]{1,0:T(8,128)(2,1)} %collective-permute-done, bf16[256,1536]{1,0:T(8,128)(2,1)S(1)} %bitcast.44), kind=kOutput, calls=%fused_computation.21 | convolution fusion | flops 806879232 | bytes 6684672 | tf_op jit(solution)/shard_map/dot_general | solution.py:250
  106.1 2.9 %fusion.8 = f32[256,2048]{1,0:T(8,128)S(1)} fusion(bf16[768,3072]{1,0:T(8,128)(2,1)} %param.6, bf16[256,1536]{1,0:T(8,128)(2,1)S(1)} %bitcast.34), kind=kOutput, calls=%fused_computation.15 | convolution fusion | flops 805306368 | bytes 5636096 | tf_op jit(solution)/shard_map/dot_general | solution.py:249
  109.0 2.0 %fusion.33 = f32[256,1024]{1,0:T(8,128)S(1)} fusion(bf16[768,3072]{1,0:T(8,128)(2,1)} %param.6, bf16[256,1536]{1,0:T(8,128)(2,1)S(1)} %bitcast.35), kind=kOutput, calls=%fused_computation.34 | convolution fusion | flops 402653184 | bytes 3014656 | tf_op jit(solution)/shard_map/dot_general | solution.py:249
  111.0 2.0 %fusion.38 = f32[256,1024]{1,0:T(8,128)S(1)} fusion(f32[256,1024]{1,0:T(8,128)S(1)} %fusion.33, bf16[768,3072]{1,0:T(8,128)(2,1)} %collective-permute-done, bf16[256,1536]{1,0:T(8,128)(2,1)S(1)} %bitcast.36), kind=kOutput, calls=%fused_computation.37 | convolution fusion | flops 403177472 | bytes 4063232 | tf_op jit(solution)/shard_map/dot_general | solution.py:250
  113.0 2.9 %fusion.13 = f32[256,2048]{1,0:T(8,128)S(1)} fusion(f32[256,2048]{1,0:T(8,128)S(1)} %fusion.8, bf16[768,3072]{1,0:T(8,128)(2,1)} %collective-permute-done, bf16[256,1536]{1,0:T(8,128)(2,1)S(1)} %bitcast.37), kind=kOutput, calls=%fused_computation.18 | convolution fusion | flops 806354944 | bytes 7733248 | tf_op jit(solution)/shard_map/dot_general | solution.py:250
  116.1 16.0 %collective-permute-done.13 = bf16[256,2048]{1,0:T(8,128)(2,1)S(1)} collective-permute-done((bf16[256,2048]{1,0:T(8,128)(2,1)}, bf16[256,2048]{1,0:T(8,128)(2,1)S(1)}, u32[]{:S(2)}, u32[]{:S(2)}) %collective-permute-start.13) | collective-permute-done | bytes 1048608 | tf_op jit(solution)/shard_map/ppermute | solution.py:24
  132.5 2.0 %pad_maximum_fusion = f32[256,3072]{1,0:T(8,128)} fusion(f32[256,2048]{1,0:T(8,128)S(1)} %convert_add_fusion, f32[256,1024]{1,0:T(8,128)S(1)} %convert_add_fusion.1), kind=kLoop, calls=%fused_computation.7 | loop fusion | flops 786432 | bytes 6291456 | tf_op jit(solution)/shard_map/concatenate | solution.py:265
  (34 shorter events, 7.8 us)
Async XLA Ops:
  0.0 51.1 %collective-permute-start = (bf16[768,3072]{1,0:T(8,128)(2,1)}, bf16[768,3072]{1,0:T(8,128)(2,1)}, u32[]{:S(2)}, u32[]{:S(2)}) collective-permute-start(bf16[768,3072]{1,0:T(8,128)(2,1)} %param.6), channel_id=1, source_target_pairs={{0,32},{32,0},{64,96},{96,64},{1,33},{33,1},{65,97},{97,65},{2,34}... | collective-permute-start | bytes 14155784 | tf_op jit(solution)/shard_map/ppermute | solution.py:24
  2.2 6.1 %copy-start.2 = (bf16[768,3072]{1,0:T(8,128)(2,1)S(1)}, bf16[768,3072]{1,0:T(8,128)(2,1)}, u32[]{:S(2)}) copy-start(bf16[768,3072]{1,0:T(8,128)(2,1)} %param.6) | copy-start | bytes 14155780
  5.4 29.9 %collective-permute-start.6 = (f16[784,768]{1,0:T(8,128)(2,1)}, f16[784,768]{1,0:T(8,128)(2,1)}, u32[]{:S(2)}, u32[]{:S(2)}) collective-permute-start(f16[784,768]{1,0:T(8,128)(2,1)} %get-tuple-element.30), channel_id=1, source_target_pairs={{0,64},{32,96},{64,0},{96,32},{1,65},{33,97},{65,1},{97,33},{2,66}... | collective-permute-start | bytes 3612680 | tf_op jit(solution)/shard_map/ppermute | solution.py:24
  18.6 30.6 %all-to-all-start = ((f16[16,384,128]{2,1,0:T(8,128)(2,1)}), f16[16,384,128]{2,1,0:T(8,128)(2,1)}, u32[]{:S(2)}, u32[]{:S(2)}) async-start(f16[16,384,128]{2,1,0:T(8,128)(2,1)} %bitcast.33), calls=%async_computation | async-start | bytes 3145728 | tf_op jit(solution)/shard_map/all_to_all | solution.py:174
  28.2 27.3 %collective-permute-start.8 = (bf16[784,768]{1,0:T(8,128)(2,1)}, bf16[784,768]{1,0:T(8,128)(2,1)}, u32[]{:S(2)}, u32[]{:S(2)}) collective-permute-start(bf16[784,768]{1,0:T(8,128)(2,1)} %get-tuple-element.27.refs_4_), channel_id=1, source_target_pairs={{0,32},{32,0},{64,96},{96,64},{1,33},{33,1},{65,97},{97,65},{2,34}... | collective-permute-start | bytes 3612680 | tf_op jit(solution)/shard_map/ppermute | solution.py:24
  28.8 31.8 %copy-start = (s32[24]{0:T(128)S(1)}, s32[24]{0:T(128)}, u32[]{:S(2)}) copy-start(s32[24]{0:T(128)} %owner_ref.1) | copy-start | bytes 292
  28.8 31.8 %copy-start.1 = (s32[24]{0:T(128)S(1)}, s32[24]{0:T(128)}, u32[]{:S(2)}) copy-start(s32[24]{0:T(128)} %live_ref.1) | copy-start | bytes 292
  28.8 26.8 %collective-permute-start.5 = (bf16[784,768]{1,0:T(8,128)(2,1)}, bf16[784,768]{1,0:T(8,128)(2,1)}, u32[]{:S(2)}, u32[]{:S(2)}) collective-permute-start(bf16[784,768]{1,0:T(8,128)(2,1)} %get-tuple-element.28.refs_0_), channel_id=1, source_target_pairs={{0,32},{32,0},{64,96},{96,64},{1,33},{33,1},{65,97},{97,65},{2,34}... | collective-permute-start | bytes 3612680 | tf_op jit(solution)/shard_map/ppermute | solution.py:24
  37.0 21.6 %collective-permute-start.9 = (bf16[784,768]{1,0:T(8,128)(2,1)S(1)}, bf16[784,768]{1,0:T(8,128)(2,1)}, u32[]{:S(2)}, u32[]{:S(2)}) collective-permute-start(bf16[784,768]{1,0:T(8,128)(2,1)S(1)} %get-tuple-element.31.refs_6_), channel_id=1, source_target_pairs={{0,32},{32,0},{64,96},{96,64},{1,33},{33,1},{65,97},{97,65},{2,34}... | collective-permute-start | bytes 3612680 | tf_op jit(solution)/shard_map/ppermute | solution.py:24
  37.9 20.6 %collective-permute-start.7 = (bf16[784,768]{1,0:T(8,128)(2,1)S(1)}, bf16[784,768]{1,0:T(8,128)(2,1)}, u32[]{:S(2)}, u32[]{:S(2)}) collective-permute-start(bf16[784,768]{1,0:T(8,128)(2,1)S(1)} %get-tuple-element.32.refs_2_), channel_id=1, source_target_pairs={{0,32},{32,0},{64,96},{96,64},{1,33},{33,1},{65,97},{97,65},{2,34}... | collective-permute-start | bytes 3612680 | tf_op jit(solution)/shard_map/ppermute | solution.py:24
  51.2 3.4 %collective-permute-start.1 = (f32[4,6,8,128]{3,2,1,0:T(8,128)S(1)}, f32[4,6,8,128]{3,2,1,0:T(8,128)S(1)}, u32[]{:S(2)}, u32[]{:S(2)}) collective-permute-start(f32[4,6,8,128]{3,2,1,0:T(8,128)S(1)} %get-tuple-element.37), channel_id=1, source_target_pairs={{0,32},{32,0},{64,96},{96,64},{1,33},{33,1},{65,97},{97,65},{2,34}... | collective-permute-start | bytes 294920 | tf_op jit(solution)/shard_map/ppermute | solution.py:24
  54.6 4.2 %collective-permute-start.4 = (f32[12,8,128]{2,1,0:T(8,128)S(1)}, f32[12,8,128]{2,1,0:T(8,128)S(1)}, u32[]{:S(2)}, u32[]{:S(2)}) collective-permute-start(f32[12,8,128]{2,1,0:T(8,128)S(1)} %get-tuple-element.33), channel_id=1, source_target_pairs={{0,65},{1,64},{2,67},{3,66},{4,69},{5,68},{6,71},{7,70},{8,73},{9,... | collective-permute-start | bytes 147464 | tf_op jit(solution)/shard_map/ppermute | solution.py:32
  55.5 3.3 %collective-permute-start.2 = (f32[12,8,128]{2,1,0:T(8,128)S(1)}, f32[12,8,128]{2,1,0:T(8,128)S(1)}, u32[]{:S(2)}, u32[]{:S(2)}) collective-permute-start(f32[12,8,128]{2,1,0:T(8,128)S(1)} %get-tuple-element.35), channel_id=1, source_target_pairs={{0,1},{1,0},{2,3},{3,2},{4,5},{5,4},{6,7},{7,6},{8,9},{9,8},{10,11... | collective-permute-start | bytes 147464 | tf_op jit(solution)/shard_map/ppermute | solution.py:32
  55.5 5.0 %collective-permute-start.3 = (f32[12,8,128]{2,1,0:T(8,128)S(1)}, f32[12,8,128]{2,1,0:T(8,128)S(1)}, u32[]{:S(2)}, u32[]{:S(2)}) collective-permute-start(f32[12,8,128]{2,1,0:T(8,128)S(1)} %get-tuple-element.36), channel_id=1, source_target_pairs={{0,64},{1,65},{2,66},{3,67},{4,68},{5,69},{6,70},{7,71},{8,72},{9,... | collective-permute-start | bytes 147464 | tf_op jit(solution)/shard_map/ppermute | solution.py:32
  69.1 17.7 %all-to-all-start.2 = ((bf16[32,12,8,128]{3,2,1,0:T(8,128)(2,1)}), bf16[32,12,8,128]{3,2,1,0:T(8,128)(2,1)S(1)}, u32[]{:S(2)}, u32[]{:S(2)}) async-start(bf16[32,12,8,128]{3,2,1,0:T(8,128)(2,1)} %get-tuple-element.22), calls=%async_computation.2 | async-start | bytes 1572864 | tf_op jit(solution)/shard_map/all_to_all | solution.py:255
  73.5 4.0 %collective-permute-start.11 = (bf16[12,8,128]{2,1,0:T(8,128)(2,1)S(1)}, bf16[12,8,128]{2,1,0:T(8,128)(2,1)S(1)}, u32[]{:S(2)}, u32[]{:S(2)}) collective-permute-start(bf16[12,8,128]{2,1,0:T(8,128)(2,1)S(1)} %get-tuple-element.19), channel_id=1, source_target_pairs={{0,65},{1,64},{2,67},{3,66},{4,69},{5,68},{6,71},{7,70},{8,73},{9,... | collective-permute-start | bytes 73736 | tf_op jit(solution)/shard_map/ppermute | solution.py:32
  75.7 7.9 %collective-permute-start.10 = (bf16[12,8,128]{2,1,0:T(8,128)(2,1)S(1)}, bf16[12,8,128]{2,1,0:T(8,128)(2,1)S(1)}, u32[]{:S(2)}, u32[]{:S(2)}) collective-permute-start(bf16[12,8,128]{2,1,0:T(8,128)(2,1)S(1)} %get-tuple-element.19), channel_id=1, source_target_pairs={{0,64},{1,65},{2,66},{3,67},{4,68},{5,69},{6,70},{7,71},{8,72},{9,... | collective-permute-start | bytes 73736 | tf_op jit(solution)/shard_map/ppermute | solution.py:32
  88.0 18.2 %all-to-all-start.1 = ((bf16[16,2,12,8,128]{4,3,2,1,0:T(8,128)(2,1)}), bf16[16,2,12,8,128]{4,3,2,1,0:T(8,128)(2,1)S(1)}, u32[]{:S(2)}, u32[]{:S(2)}) async-start(bf16[16,2,12,8,128]{4,3,2,1,0:T(8,128)(2,1)} %broadcast_in_dim.23), calls=%async_computation.1 | async-start | bytes 1572864 | tf_op jit(solution)/shard_map/all_to_all | solution.py:56
  96.4 19.6 %collective-permute-start.12 = (bf16[256,1024]{1,0:T(8,128)(2,1)}, bf16[256,1024]{1,0:T(8,128)(2,1)S(1)}, u32[]{:S(2)}, u32[]{:S(2)}) collective-permute-start(bf16[256,1024]{1,0:T(8,128)(2,1)} %fusion.47), channel_id=1, source_target_pairs={{0,64},{32,96},{64,0},{96,32},{1,65},{33,97},{65,1},{97,33},{2,66}... | collective-permute-start | bytes 1572872 | tf_op jit(solution)/shard_map/ppermute | solution.py:24
  105.3 26.9 %collective-permute-start.13 = (bf16[256,2048]{1,0:T(8,128)(2,1)}, bf16[256,2048]{1,0:T(8,128)(2,1)S(1)}, u32[]{:S(2)}, u32[]{:S(2)}) collective-permute-start(bf16[256,2048]{1,0:T(8,128)(2,1)} %fusion.22), channel_id=1, source_target_pairs={{0,64},{32,96},{64,0},{96,32},{1,65},{33,97},{65,1},{97,33},{2,66}... | collective-permute-start | bytes 3145736 | tf_op jit(solution)/shard_map/ppermute | solution.py:24
